TPU v7x, 32 devices: a whole 2x2x4 slice. The times are simulated.
32 devices in a mesh: groups: 1, tensor: 32 (over z, y, x, core).
Axes of the slice: x: 2, y: 2, z: 4, core: 2. Of those that a mesh axis runs over, the one named last changes fastest.
Arguments:
- hidden_in: bfloat16 [4, 16384], P('groups', 'tensor'), may hold values from -0.59765625 to 0.59765625
- norm_gain: bfloat16 [16384], P('tensor'), may hold values from 0.5 to 1.5
- w_q: bfloat16 [16384, 16384], P('tensor'), may hold values from -1 to 256
- w_kv: bfloat16 [16384, 2048], P('tensor'), may hold values from -0.046875 to 0.046875
- w_o: bfloat16 [16384, 16384], P(None, 'tensor'), may hold values from -0.046875 to 0.046875
- kv_cache: bfloat16 [8, 4, 2, 4096, 128], P(None, 'groups', None, 'tensor'), may hold values from -8 to 8
- lengths: int32 [4], P('groups'), may hold values from 2 to 4096, as said below
- slab_index: int32 [8, 4], P(None, 'groups'), may hold values from 0 to 3, each once within a row
Outputs:
- hidden_out: bfloat16 [4, 16384], P('groups', 'tensor')
Inputs may be any that keep to these rules, and one draw needn't show every extreme that they name: `lengths`: one request in every draw has exactly 4096 cached tokens.
All inputs are finite; a program needn't handle non-finite values.
Results may differ from a plain program's by a relative error of at most 0.0085.
The roundings to bfloat16 on the way count: a program that leaves them out, or rounds other values in their place, can miss the bound.
Values may be sent and summed in bfloat16 or wider, within the bound.
A program may use at most 128 MiB of HBM per device.

v0:
```python
import jax
import jax.numpy as jnp
from jax import lax
from jax.sharding import PartitionSpec as P

KVH = 8
HD = 128
GROUP = 16


epsilon = 1e-05
rope_base = 500000.0


def rotate(values, position):
    head_dim = values.shape[-1]
    half_dim = head_dim // 2
    frequency = rope_base ** (-2.0 * jnp.arange(half_dim, dtype=jnp.float32) / head_dim)
    angles = position[..., None] * frequency
    cosine = jnp.cos(angles)
    sines = jnp.sin(angles)
    lower_half = values[..., :half_dim]
    upper_half = values[..., half_dim:]
    return jnp.concatenate(
        [lower_half * cosine - upper_half * sines, upper_half * cosine + lower_half * sines],
        axis=-1,
    )


def body(hidden_in, norm_gain, w_q, w_kv, w_o, kv_cache, lengths, slab_index):
    my_index = lax.axis_index("tensor")
    requests = hidden_in.shape[0]
    model_width = KVH * GROUP * HD
    query_width = GROUP * HD
    stream = hidden_in.astype(jnp.float32)
    squares = lax.psum(jnp.sum(stream * stream, axis=1), "tensor")
    normed = (
        stream * lax.rsqrt(squares[:, None] / model_width + epsilon) * norm_gain.astype(jnp.float32)
    ).astype(jnp.bfloat16)
    part_q = jnp.dot(normed, w_q, preferred_element_type=jnp.float32)
    part_kv = jnp.dot(normed, w_kv, preferred_element_type=jnp.float32)
    counter = jnp.arange(requests, dtype=jnp.int32)
    slab_match = (slab_index[:, None, :] == counter[None, :, None]).astype(jnp.int32)
    inverse = jnp.sum(slab_match * counter[None, None, :], axis=2)
    kv_rows = jnp.transpose(part_kv.reshape(requests, 2, KVH, HD), (0, 2, 1, 3)).reshape(
        requests, KVH, 2 * HD
    )
    proj_rows = jnp.concatenate([part_q.reshape(requests, KVH, query_width), kv_rows], axis=2)
    proj_rows = jnp.take_along_axis(
        jnp.transpose(proj_rows, (1, 0, 2)), inverse[:, :, None], axis=1
    )
    proj_rows = proj_rows.reshape(KVH * requests, query_width + 2 * HD)
    my_row = lax.psum_scatter(proj_rows, "tensor", scatter_dimension=0, tiled=True)[0]
    slab_pos = my_index % requests
    head_pos = my_index // requests
    request = inverse[head_pos, slab_pos]
    length = lengths[request]
    position = length.astype(jnp.float32)
    q_row = rotate(my_row[:query_width].reshape(GROUP, HD), position).astype(jnp.bfloat16)
    k_row = rotate(my_row[query_width : query_width + HD], position).astype(jnp.bfloat16)
    v_row = my_row[query_width + HD :].astype(jnp.bfloat16)
    score_scale = 1.0 / HD**0.5
    local_cache = kv_cache.reshape(KVH * kv_cache.shape[1], 2, kv_cache.shape[3], HD)
    slab_data = lax.all_to_all(local_cache, "tensor", split_axis=0, concat_axis=2, tiled=True)[0]
    full_len = slab_data.shape[1]
    scores = (
        jnp.einsum("gd,pd->gp", q_row, slab_data[0], preferred_element_type=jnp.float32)
        * score_scale
    )
    new_score = jnp.dot(q_row, k_row, preferred_element_type=jnp.float32) * score_scale
    visible = jnp.arange(full_len, dtype=jnp.int32)[None, :] < length
    row_max = jnp.maximum(jnp.max(jnp.where(visible, scores, -1e30), axis=1), new_score)
    weights = jnp.where(visible, jnp.exp(scores - row_max[:, None]), 0.0)
    new_weight = jnp.exp(new_score - row_max)
    denominator = jnp.sum(weights, axis=1) + new_weight
    weighted = jnp.dot(
        weights.astype(jnp.bfloat16), slab_data[1], preferred_element_type=jnp.float32
    )
    weighted = (
        weighted
        + new_weight.astype(jnp.bfloat16).astype(jnp.float32)[:, None]
        * v_row.astype(jnp.float32)[None, :]
    )
    out_row = (weighted / denominator[:, None]).astype(jnp.bfloat16).reshape(1, query_width)
    gathered = lax.all_gather(out_row, "tensor", axis=0, tiled=True)
    ordered = jnp.take_along_axis(
        gathered.reshape(KVH, requests, query_width), slab_index[:, :, None], axis=1
    )
    attention = jnp.transpose(ordered, (1, 0, 2)).reshape(requests, model_width)
    result = stream + jnp.dot(attention, w_o, preferred_element_type=jnp.float32)
    return result.astype(jnp.bfloat16)


def solution(mesh):
    placed = (
        P("groups", "tensor"),
        P("tensor"),
        P("tensor", None),
        P("tensor", None),
        P(None, "tensor"),
        P(None, "groups", None, "tensor", None),
        P("groups"),
        P(None, "groups"),
    )
    return jax.shard_map(
        body, mesh=mesh, in_specs=placed, out_specs=P("groups", "tensor"), check_vma=False
    )
```

profile of v0, /device:TPU:0, one launch (start us, length us, event | category | flops | bytes accessed | tf_op | source)
XLA Modules:
  0.0 287.7 jit_solution(17600641808804767192)
XLA Ops:
  6.5 7.5 %all-to-all-start = ((bf16[32,2,128,128]{3,2,1,0:T(8,128)(2,1)}), bf16[32,2,128,128]{3,2,1,0:T(8,128)(2,1)}, u32[]{:S(2)}, u32[]{:S(2)}) async-start(bf16[32,2,128,128]{3,2,1,0:T(8,128)(2,1)} %bitcast.70), calls=%async_computation | async-start | bytes 4194304 | tf_op jit(solution)/shard_map/all_to_all | solution.py:64
  14.1 0.8 fusion.10
  14.9 0.7 convert_element_type.35
  15.5 67.7 %psum.7 = f32[4]{0:T(128)S(1)} all-reduce(f32[4]{0:T(128)S(1)} %fusion.10), channel_id=1, replica_groups=mesh['groups'=1,'tensor'=32] {'tensor'}, use_global_device_ids=true, to_apply=%region_2.0 | all-reduce | flops 4 | bytes 32 | tf_op jit(solution)/shard_map/psum | solution.py:36
  83.3 1.2 convolution_bitcast_fusion
  84.5 0.7 select_reduce_fusion.1
  85.6 8.1 %fusion.27 = f32[4,16384]{1,0:T(4,128)S(1)} fusion(bf16[512,16384]{1,0:T(8,128)(2,1)} %param.10, bf16[4,512]{1,0:T(4,128)(2,1)} %param.8, f32[512]{0:T(512)S(1)} %convert_element_type.35, f32[4]{0:T(128)S(1)} %add_rsqrt_fusion), kind=kOutput, calls=%fused_computation.64 | convolution fusion | flops 67117056 | bytes 17045520 | tf_op jit(solution)/shard_map/dot_general | solution.py:40
  93.7 1.0 gather_fusion
  94.8 0.8 broadcast_select_fusion
  95.6 0.6 dynamic_slice.6
  98.2 0.6 dynamic_slice.7
  99.8 0.7 iota_compare_fusion
  100.4 121.9 %all-reduce.3.cloned.1.call-done = f32[32,2304]{1,0:T(8,128)} async-done(((f32[32,2304]{1,0:T(8,128)}), f32[32,2304]{1,0:T(8,128)}) %all-reduce.3.cloned.1.call-update) | async-done | bytes 294928
  222.3 0.8 fusion.17
  223.0 0.8 subtract_convert_fusion.1
  223.9 0.9 constant_dynamic-slice_fusion
  224.8 1.7 fusion.29
  226.5 0.5 select_reduce_fusion
  227.3 0.3 fusion.4
  227.5 0.3 fusion.2
  227.9 42.2 %all-gather = bf16[32,1,2048]{2,1,0:T(2,128)(2,1)S(1)} all-gather(bf16[1,1,2048]{2,1,0:T(2,128)(2,1)S(1)} %reshape.120), channel_id=1, replica_groups=mesh['groups'=1,'tensor'=32] {'tensor'}, dimensions={0}, use_global_device_ids=true | all-gather | bytes 135168 | tf_op jit(solution)/shard_map/all_gather | solution.py:85
  270.1 0.8 reduce
  271.0 1.0 gather_fusion.1
  272.2 8.6 %fusion.1 = bf16[4,512]{1,0:T(4,128)(2,1)} fusion(bf16[4,16384]{1,0:T(4,128)(2,1)S(1)} %bitcast.72, bf16[16384,512]{1,0:T(8,128)(2,1)} %param.12, bf16[4,512]{1,0:T(4,128)(2,1)S(1)} %copy-done.1), kind=kOutput, calls=%fused_computation.7 | convolution fusion | flops 67115008 | bytes 16916480 | tf_op jit(solution)/shard_map/dot_general | solution.py:90
  (35 shorter events, 1.4 us)
Async XLA Ops:
  6.5 76.7 %copy-start = (bf16[512,2048]{1,0:T(8,128)(2,1)S(1)}, bf16[512,2048]{1,0:T(8,128)(2,1)}, u32[]{:S(2)}) copy-start(bf16[512,2048]{1,0:T(8,128)(2,1)} %param.11) | copy-start | bytes 6291460
  6.5 92.9 %copy-start.2 = (s32[8,4]{0,1:T(4,128)S(1)}, s32[8,4]{0,1:T(4,128)}, u32[]{:S(2)}) copy-start(s32[8,4]{0,1:T(4,128)} %param.15) | copy-start | bytes 388
  6.5 91.6 %copy-start.3 = (s32[4]{0:T(128)S(1)}, s32[4]{0:T(128)}, u32[]{:S(2)}) copy-start(s32[4]{0:T(128)} %param.14) | copy-start | bytes 52
  6.5 218.3 %all-to-all-start = ((bf16[32,2,128,128]{3,2,1,0:T(8,128)(2,1)}), bf16[32,2,128,128]{3,2,1,0:T(8,128)(2,1)}, u32[]{:S(2)}, u32[]{:S(2)}) async-start(bf16[32,2,128,128]{3,2,1,0:T(8,128)(2,1)} %bitcast.70), calls=%async_computation | async-start | bytes 4194304 | tf_op jit(solution)/shard_map/all_to_all | solution.py:64
  14.0 208.3 %all-reduce.3.cloned.1.call-start = ((), (), s32[]{:S(2)}) async-start(), calls=%async_computation.1 | async-start | bytes 589824
  83.3 188.9 %copy-start.1 = (bf16[4,512]{1,0:T(4,128)(2,1)S(1)}, bf16[4,512]{1,0:T(4,128)(2,1)}, u32[]{:S(2)}) copy-start(bf16[4,512]{1,0:T(4,128)(2,1)} %param.8) | copy-start | bytes 12292
Sparse Core Ops, SparseCore 0:
  95.7 126.5 all-reduce.2
where the time goes:
time: 288 us
  waiting for transfers between devices  122 us (42%)
  blocking collectives  110 us (38%)
  matrix products  19 us (7%)
  between operations  16.2 us (6%)
  starting transfers between devices  7.5 us (3%)
  other arithmetic  6.67 us (2%)
  local copies, waits for them, and re-layouts  6.55 us (2%)
    unnamed x2, waiting for transfers between devices  122 us
    psum x1, blocking collectives, body(): squares = lax.psum(jnp.sum(stream * stream, axis=1), 'tensor')  67.7 us
    all_gather x1, blocking collectives, body(): gathered = lax.all_gather(out_row, 'tensor', axis=0, tiled=True)  42.2 us
    dot_general x1, matrix products, body(): jnp.dot(attention, w_o, preferred_element_type=jnp.float32)  8.64 us
    dot_general x1, matrix products, body(): part_q = jnp.dot(normed, w_q, preferred_element_type=jnp.float32)  8.1 us
    all_to_all x1, starting transfers between devices, body(): lax.all_to_all(local_cache, 'tensor', split_axis=0, concat_axis=2, tiled=...  7.45 us
  transfers between devices with their start and end apart: 2, of which 1 were waited for; matrix products, arithmetic and copies ran while one was open for 6% of the time, Pallas kernels for 0%

commit v1 on v0

v1 whole, which is shorter than its diff:
```python
import functools

import jax
import jax.numpy as jnp
from jax import lax
from jax.experimental import pallas as pl
from jax.experimental.pallas import tpu as pltpu
from jax.sharding import PartitionSpec as P

KVH = 8
HD = 128
GROUP = 16

epsilon = 1e-05
rope_base = 500000.0
score_scale = 1.0 / HD**0.5
lowest = -1e30


def step_kernel(
    n,
    slab_ref,
    len_ref,
    hidden_ref,
    gain_ref,
    cos_ref,
    sin_ref,
    wq_hbm,
    wkv_hbm,
    wo_hbm,
    kv_hbm,
    out_ref,
    wq_v,
    wkv_v,
    wo_v,
    kv_v,
    sq_buf,
    kvp,
    part_buf,
    part_in,
    q_buf,
    fin,
    k_rows,
    v_rows,
    o_buf,
    o_in,
    st_buf,
    st_in,
    att_f,
    att_buf,
    wq_sem,
    wkv_sem,
    wo_sem,
    kv_sem,
    send_sem,
    recv_sem,
    att_sem,
):
    me = lax.axis_index("tensor")
    requests, width = hidden_ref.shape
    heads = KVH * GROUP // n
    cols = heads * HD
    q_rows = heads * requests
    per_kv = GROUP // heads
    slabs, positions = kv_v.shape[1], kv_v.shape[3]

    def wq_copy(step):
        owner = lax.rem(me + 1 + step, n)
        return pltpu.make_async_copy(
            wq_hbm.at[:, pl.ds(pl.multiple_of(owner * cols, cols), cols)],
            wq_v.at[step],
            wq_sem.at[step],
        )

    wkv_copy = pltpu.make_async_copy(wkv_hbm, wkv_v, wkv_sem)
    wo_copy = pltpu.make_async_copy(wo_hbm, wo_v, wo_sem)
    kv_copy = pltpu.make_async_copy(kv_hbm, kv_v, kv_sem)
    wkv_copy.start()

    @pl.loop(0, n)
    def _(step):
        wq_copy(step).start()

    def remote(src, dst, phase, peer):
        return pltpu.make_async_remote_copy(
            src_ref=src,
            dst_ref=dst,
            send_sem=send_sem.at[phase],
            recv_sem=recv_sem.at[phase],
            device_id={"tensor": peer},
            device_id_type=pl.DeviceIdType.MESH,
        )

    def wait_all(buf, phase, sent=True, received=True):
        every = buf.at[pl.ds(0, n - 1)]
        descriptor = remote(every, every, phase, lax.rem(me + 1, n))
        if received:
            descriptor.wait_recv()
        if sent:
            descriptor.wait_send()

    barrier = pltpu.get_barrier_semaphore()

    @pl.loop(1, n)
    def _(step):
        pl.semaphore_signal(
            barrier,
            inc=1,
            device_id={"tensor": lax.rem(me + step, n)},
            device_id_type=pl.DeviceIdType.MESH,
        )

    stream = hidden_ref[...].astype(jnp.float32)
    own_sq = jnp.sum(stream * stream, axis=1, keepdims=True)
    sq_buf[me] = jnp.broadcast_to(own_sq, (requests, HD))
    pl.semaphore_wait(barrier, n - 1)

    @pl.loop(1, n)
    def _(step):
        remote(sq_buf.at[me], sq_buf.at[me], 0, lax.rem(me + step, n)).start()

    wait_all(sq_buf, 0)
    squares = jnp.sum(sq_buf[...], axis=0)[:, :1]
    normed = (
        stream
        * lax.rsqrt(squares / (width * n) + epsilon)
        * gain_ref[...].astype(jnp.float32)
    ).astype(jnp.bfloat16)

    wkv_copy.wait()
    for piece in range(2 * KVH * HD // 512):
        res = jnp.dot(
            normed, wkv_v[:, piece * 512 : (piece + 1) * 512], preferred_element_type=jnp.float32
        )
        for j in range(4):
            kvp[piece * 4 + j] = res[:, j * HD : (j + 1) * HD]

    def project(step, target):
        owner = lax.rem(me + 1 + step, n)
        wq_copy(step).wait()
        res = jnp.dot(normed, wq_v[step], preferred_element_type=jnp.float32)
        for j in range(heads):
            target[j * requests : (j + 1) * requests, :] = res[:, j * HD : (j + 1) * HD]
        kv_head = owner // per_kv
        target[q_rows : q_rows + requests, :] = kvp[kv_head]
        target[q_rows + requests : q_rows + 2 * requests, :] = kvp[KVH + kv_head]
        return owner

    @pl.loop(0, n - 1)
    def _(step):
        owner = project(step, part_buf.at[step])
        remote(part_buf.at[step], part_in.at[me], 1, owner).start()

    kv_copy.start()
    wo_copy.start()
    project(n - 1, part_in.at[me])
    wait_all(part_in, 1)

    total = jnp.sum(part_in[...], axis=0)
    total = total * cos_ref[...] + pltpu.roll(total, HD // 2, 1) * sin_ref[...]
    rounded = total.astype(jnp.bfloat16)
    fin[...] = rounded.astype(jnp.float32)
    q_buf[me] = fin[:q_rows, :].astype(jnp.bfloat16)

    @pl.loop(1, n)
    def _(step):
        remote(q_buf.at[me], q_buf.at[me], 2, lax.rem(me + step, n)).start()

    for j in range(heads):
        k_rows[j * requests : (j + 1) * requests, :] = fin[q_rows : q_rows + requests, :]
        v_rows[j * requests : (j + 1) * requests, :] = fin[
            q_rows + requests : q_rows + 2 * requests, :
        ]
    new_score = jnp.sum(fin[:q_rows, :] * k_rows[...], axis=1, keepdims=True) * score_scale
    lane = lax.broadcasted_iota(jnp.int32, (q_rows, HD), 1)
    row = lax.broadcasted_iota(jnp.int32, (q_rows, HD), 0)
    diagonal = lane == row
    shifted = lane == row + HD // 2
    new_lane = jnp.sum(jnp.where(diagonal, new_score, 0.0), axis=0, keepdims=True)

    all_rows = GROUP * requests
    keys = slabs * positions
    row_req = lax.rem(lax.broadcasted_iota(jnp.int32, (all_rows, 1), 0), requests)
    column = lax.broadcasted_iota(jnp.int32, (1, keys), 1)
    column_slab = column // positions
    column_pos = lax.rem(column, positions) + me * positions
    row_len = jnp.zeros((all_rows, 1), jnp.int32)
    for b in range(requests):
        row_len = jnp.where(row_req == b, len_ref[b], row_len)
    in_length = column_pos < row_len

    kv_copy.wait()
    wait_all(q_buf, 2)

    @pl.loop(0, KVH)
    def _(h):
        row_slab = jnp.zeros((all_rows, 1), jnp.int32)
        for b in range(requests):
            row_slab = jnp.where(row_req == b, slab_ref[h, b], row_slab)
        visible = jnp.logical_and(column_slab == row_slab, in_length)
        queries = q_buf[pl.ds(h * per_kv, per_kv)].reshape(all_rows, HD)
        key_block = kv_v[h, :, 0].reshape(keys, HD)
        value_block = kv_v[h, :, 1].reshape(keys, HD)
        scores = (
            lax.dot_general(
                queries, key_block, (((1,), (1,)), ((), ())), preferred_element_type=jnp.float32
            )
            * score_scale
        )
        scores = jnp.where(visible, scores, lowest)
        top = jnp.max(scores, axis=1, keepdims=True)
        weights = jnp.where(visible, jnp.exp(scores - top), 0.0)
        weight_sum = jnp.sum(weights, axis=1, keepdims=True)
        weighted = jnp.dot(
            weights.astype(jnp.bfloat16), value_block, preferred_element_type=jnp.float32
        )
        for t in range(per_kv):
            owner = h * per_kv + t
            own = slice(t * q_rows, (t + 1) * q_rows)
            o_buf[owner] = weighted[own].astype(jnp.bfloat16)
            st_buf[owner] = jnp.sum(
                jnp.where(diagonal, top[own], 0.0) + jnp.where(shifted, weight_sum[own], 0.0),
                axis=0,
                keepdims=True,
            )

    o_in[me] = o_buf[me]
    st_in[me] = st_buf[me]

    @pl.loop(1, n)
    def _(step):
        peer = lax.rem(me + step, n)
        remote(st_buf.at[peer], st_in.at[me], 3, peer).start()
        remote(o_buf.at[peer], o_in.at[me], 4, peer).start()

    wait_all(st_in, 3)
    stats = st_in[...]
    top_lane = jnp.maximum(jnp.max(stats, axis=0), new_lane)
    factor = jnp.exp(jnp.minimum(stats - top_lane[None], 0.0))
    new_factor = jnp.exp(new_lane - top_lane)
    sums = jnp.concatenate([stats[:, :, HD // 2 :], stats[:, :, : HD // 2]], axis=2)
    denominator_lane = jnp.sum(factor * sums, axis=0) + new_factor

    def as_column(lanes):
        return jnp.sum(jnp.where(diagonal, lanes, 0.0), axis=1, keepdims=True)

    wait_all(o_in, 4)
    weighted = as_column(new_factor).astype(jnp.bfloat16).astype(jnp.float32) * v_rows[...]
    columns = jnp.sum(jnp.where(diagonal[None], factor, 0.0), axis=2, keepdims=True)
    weighted = weighted + jnp.sum(columns * o_in[...].astype(jnp.float32), axis=0)
    att_f[...] = weighted / as_column(denominator_lane)
    for j in range(heads):
        att_buf[me, :, j * HD : (j + 1) * HD] = att_f[
            j * requests : (j + 1) * requests, :
        ].astype(jnp.bfloat16)

    def att_copy(peer, source):
        return pltpu.make_async_remote_copy(
            src_ref=att_buf.at[source],
            dst_ref=att_buf.at[source],
            send_sem=send_sem.at[5],
            recv_sem=att_sem.at[source],
            device_id={"tensor": peer},
            device_id_type=pl.DeviceIdType.MESH,
        )

    @pl.loop(1, n)
    def _(step):
        att_copy(lax.rem(me + step, n), me).start()

    wo_copy.wait()

    def project_out(source):
        return jnp.dot(
            att_buf[source],
            wo_v[pl.ds(pl.multiple_of(source * cols, cols), cols), :],
            preferred_element_type=jnp.float32,
        )

    def add(step, acc):
        source = lax.rem(me + n - step, n)
        att_copy(lax.rem(me + 1, n), source).wait_recv()
        return acc + project_out(source)

    acc = lax.fori_loop(1, n, add, project_out(me))
    out_ref[...] = (stream + acc).astype(jnp.bfloat16)
    wait_all(att_buf, 5, received=False)


def body(n, hidden_in, norm_gain, w_q, w_kv, w_o, kv_cache, lengths, slab_index):
    requests, width = hidden_in.shape
    heads = KVH * GROUP // n
    cols = heads * HD
    q_rows = heads * requests
    all_rows = q_rows + 2 * requests
    slabs, positions = kv_cache.shape[1], kv_cache.shape[3]

    half = HD // 2
    frequency = rope_base ** (-2.0 * jnp.arange(half, dtype=jnp.float32) / HD)
    angles = lengths.astype(jnp.float32)[:, None] * frequency
    cosine, sine = jnp.cos(angles), jnp.sin(angles)
    cosine = jnp.concatenate([cosine, cosine], axis=1)
    sine = jnp.concatenate([-sine, sine], axis=1)
    cosine = jnp.concatenate([jnp.tile(cosine, (heads + 1, 1)), jnp.ones_like(cosine)], axis=0)
    sine = jnp.concatenate([jnp.tile(sine, (heads + 1, 1)), jnp.zeros_like(sine)], axis=0)

    vmem = pl.BlockSpec(memory_space=pltpu.VMEM)
    smem = pl.BlockSpec(memory_space=pltpu.SMEM)
    hbm = pl.BlockSpec(memory_space=pl.ANY)
    bf16, f32 = jnp.bfloat16, jnp.float32
    return pl.pallas_call(
        functools.partial(step_kernel, n),
        out_shape=jax.ShapeDtypeStruct((requests, width), bf16),
        in_specs=[smem, smem, vmem, vmem, vmem, vmem, hbm, hbm, hbm, hbm],
        out_specs=vmem,
        scratch_shapes=[
            pltpu.VMEM((n, width, cols), bf16),
            pltpu.VMEM(w_kv.shape, bf16),
            pltpu.VMEM(w_o.shape, bf16),
            pltpu.VMEM(kv_cache.shape, bf16),
            pltpu.VMEM((n, requests, HD), f32),
            pltpu.VMEM((2 * KVH, requests, HD), f32),
            pltpu.VMEM((n - 1, all_rows, HD), f32),
            pltpu.VMEM((n, all_rows, HD), f32),
            pltpu.VMEM((n, q_rows, HD), bf16),
            pltpu.VMEM((all_rows, HD), f32),
            pltpu.VMEM((q_rows, HD), f32),
            pltpu.VMEM((q_rows, HD), f32),
            pltpu.VMEM((n, q_rows, HD), bf16),
            pltpu.VMEM((n, q_rows, HD), bf16),
            pltpu.VMEM((n, 1, HD), f32),
            pltpu.VMEM((n, 1, HD), f32),
            pltpu.VMEM((q_rows, HD), f32),
            pltpu.VMEM((n, requests, cols), bf16),
            pltpu.SemaphoreType.DMA((n,)),
            pltpu.SemaphoreType.DMA,
            pltpu.SemaphoreType.DMA,
            pltpu.SemaphoreType.DMA,
            pltpu.SemaphoreType.DMA((6,)),
            pltpu.SemaphoreType.DMA((5,)),
            pltpu.SemaphoreType.DMA((n,)),
        ],
        compiler_params=pltpu.CompilerParams(
            collective_id=0, has_side_effects=True, vmem_limit_bytes=56 * 1024 * 1024
        ),
    )(
        slab_index,
        lengths,
        hidden_in,
        norm_gain.reshape(1, width),
        cosine,
        sine,
        w_q,
        w_kv,
        w_o,
        kv_cache,
    )


def solution(mesh):
    placed = (
        P("groups", "tensor"),
        P("tensor"),
        P("tensor", None),
        P("tensor", None),
        P(None, "tensor"),
        P(None, "groups", None, "tensor", None),
        P("groups"),
        P(None, "groups"),
    )
    return jax.shard_map(
        functools.partial(body, mesh.shape["tensor"]),
        mesh=mesh,
        in_specs=placed,
        out_specs=P("groups", "tensor"),
        check_vma=False,
    )
```

time: 288 us -> 56.9 us (0.20)
  waiting for transfers between devices: 122 us -> 0 us
  blocking collectives: 110 us -> 0 us
  Pallas kernels: 0 us -> 50.7 us
  matrix products: 19 us -> 0 us
  between operations: 16.2 us -> 0.02 us
  starting transfers between devices: 7.5 us -> 0 us
  other arithmetic: 6.67 us -> 0.85 us
    unnamed x2 -> x0, waiting for transfers between devices: 122 us -> none
    psum x1 -> x0, blocking collectives: 67.7 us -> none  [body(): squares = lax.psum(jnp.sum(stream * stream, axis=1), 'tensor')]
    pallas_call x0 -> x1, Pallas kernels: none -> 50.7 us  [body(): pl.pallas_call(functools.partial(step_kernel, n), out_shape=jax.ShapeDtyp...]
    all_gather x1 -> x0, blocking collectives: 42.2 us -> none  [body(): gathered = lax.all_gather(out_row, 'tensor', axis=0, tiled=True)]
    dot_general x6 -> x0, matrix products: 19 us -> none  [the longest x1 8.64 us: body(): jnp.dot(attention, w_o, preferred_element_type=jnp.float32)]
    all_to_all x1 -> x0, starting transfers between devices: 7.45 us -> none  [body(): lax.all_to_all(local_cache, 'tensor', split_axis=0, concat_axis=2, tiled=...]
  transfers between devices with their start and end apart: 2 -> 0, of which waited for: 1 -> 0; matrix products, arithmetic and copies ran while one was open for 6% -> 0% of each run, Pallas kernels for 0% -> 0%
where the time goes in v1:
time: 56.9 us; the launch traced here: 56.7 us
  Pallas kernels  50.7 us (89%)
  local copies, waits for them, and re-layouts  5.12 us (9%)
  other arithmetic  0.85 us (1%)
    pallas_call x1, Pallas kernels, body(): pl.pallas_call(functools.partial(step_kernel, n), out_shape=jax.ShapeDtyp...  50.7 us
    unnamed x2, local copies, waits for them, and re-layouts  2.62 us
    reshape x1, local copies, waits for them, and re-layouts, body(): norm_gain.reshape(1, width)  1.26 us

profile of v1, /device:TPU:0, one launch (start us, length us, event | category | flops | bytes accessed | tf_op | source)
XLA Modules:
  0.0 56.7 jit_solution(13965873562425619136)
XLA Ops:
  0.0 0.7 %convert_element_type.3 = f32[4]{0:T(128)S(1)} convert(s32[4]{0:T(128)} %len_ref.1) | non-fusion elementwise | flops 4 | bytes 32 | tf_op jit(solution)/shard_map/convert_element_type | solution.py:300
  0.7 0.1 fusion
  0.8 0.1 pad_maximum_fusion
  0.9 0.6 %concatenate.13.cos_ref = f32[24,128]{1,0:T(8,128)} pad(f32[20,128]{1,0:T(8,128)S(1)} %tile.9, f32[]{:T(128)} %constant.3.clone.1), padding=0_4x0_0 | pad | bytes 22532 | tf_op jit(solution)/shard_map/concatenate | solution.py:304
  1.5 0.6 %concatenate.15.sin_ref = f32[24,128]{1,0:T(8,128)} pad(f32[20,128]{1,0:T(8,128)S(1)} %tile.21, f32[]{:T(128)} %constant.10.clone.1), padding=0_4x0_0 | pad | bytes 22532 | tf_op jit(solution)/shard_map/concatenate | solution.py:305
  2.1 1.3 %copy.9.slab_ref = s32[8,4]{1,0:T(8,128)} copy(s32[8,4]{0,1:T(4,128)} %param.15) | data formatting | bytes 256 | tf_op args[7]
  3.5 1.3 %reshape.17.gain_ref = bf16[1,512]{1,0:T(2,128)(2,1)} reshape(bf16[512]{0:T(512)(128)(2,1)} %param.9) | data formatting | bytes 2048 | tf_op jit(solution)/shard_map/reshape | solution.py:350
  4.7 50.7 %shard_map.82 = bf16[4,512]{1,0:T(4,128)(2,1)} custom-call(s32[8,4]{1,0:T(8,128)} %copy.9.slab_ref, s32[4]{0:T(128)} %len_ref.1, bf16[4,512]{1,0:T(4,128)(2,1)} %hidden_ref.1, bf16[1,512]{1,0:T(2,128)(2,1)} %reshape.17.gain_ref, f32[24,128]{1,0:T(8,128)} %concatenate.13.cos_ref, f32[24,128]{1,0:T(8,128)} %concatenate.15.sin_ref, bf16[512,16384]{1,0:T(8,128)(2,1)} %wq_hbm.1, ...), custom_call_target="tpu_custom_call" | custom-call | tf_op jit(solution)/shard_map/pallas_call | solution.py:311
  55.4 1.3 %copy.11 = bf16[4,512]{1,0:T(4,128)(2,1)} copy(bf16[4,512]{1,0:T(4,128)(2,1)} %shard_map.82) | data formatting | bytes 8192
  (5 shorter events, 0.0 us)

commit v2 on v1

--- a/solution.py
+++ b/solution.py
@@ -146,7 +146,7 @@
         target[q_rows + requests : q_rows + 2 * requests, :] = kvp[KVH + kv_head]
         return owner
 
-    @pl.loop(0, n - 1)
+    @pl.loop(0, n - 1, unroll=True)
     def _(step):
         owner = project(step, part_buf.at[step])
         remote(part_buf.at[step], part_in.at[me], 1, owner).start()
@@ -192,7 +192,7 @@
     kv_copy.wait()
     wait_all(q_buf, 2)
 
-    @pl.loop(0, KVH)
+    @pl.loop(0, KVH, unroll=True)
     def _(h):
         row_slab = jnp.zeros((all_rows, 1), jnp.int32)
         for b in range(requests):

time: 56.9 us -> 56 us (0.984)
  Pallas kernels: 50.7 us -> 49.7 us
    pallas_call x1, Pallas kernels: 50.7 us -> 49.7 us  [body(): pl.pallas_call(functools.partial(step_kernel, n), out_shape=jax.ShapeDtyp...]
where the time goes in v2:
time: 56 us; the launch traced here: 55.7 us
  Pallas kernels  49.7 us (89%)
  local copies, waits for them, and re-layouts  5.12 us (9%)
  other arithmetic  0.85 us (2%)
    pallas_call x1, Pallas kernels, body(): pl.pallas_call(functools.partial(step_kernel, n), out_shape=jax.ShapeDtyp...  49.7 us
    unnamed x2, local copies, waits for them, and re-layouts  2.62 us
    reshape x1, local copies, waits for them, and re-layouts, body(): norm_gain.reshape(1, width)  1.26 us

profile of v2, /device:TPU:0, one launch (start us, length us, event | category | flops | bytes accessed | tf_op | source)
XLA Modules:
  0.0 55.7 jit_solution(4582487716170893653)
XLA Ops:
  0.0 0.7 %convert_element_type.3 = f32[4]{0:T(128)S(1)} convert(s32[4]{0:T(128)} %len_ref.1) | non-fusion elementwise | flops 4 | bytes 32 | tf_op jit(solution)/shard_map/convert_element_type | solution.py:300
  0.7 0.1 fusion
  0.8 0.1 pad_maximum_fusion
  0.9 0.6 %concatenate.13.cos_ref = f32[24,128]{1,0:T(8,128)} pad(f32[20,128]{1,0:T(8,128)S(1)} %tile.9, f32[]{:T(128)} %constant.3.clone.1), padding=0_4x0_0 | pad | bytes 22532 | tf_op jit(solution)/shard_map/concatenate | solution.py:304
  1.5 0.6 %concatenate.15.sin_ref = f32[24,128]{1,0:T(8,128)} pad(f32[20,128]{1,0:T(8,128)S(1)} %tile.21, f32[]{:T(128)} %constant.10.clone.1), padding=0_4x0_0 | pad | bytes 22532 | tf_op jit(solution)/shard_map/concatenate | solution.py:305
  2.1 1.3 %copy.9.slab_ref = s32[8,4]{1,0:T(8,128)} copy(s32[8,4]{0,1:T(4,128)} %param.15) | data formatting | bytes 256 | tf_op args[7]
  3.5 1.3 %reshape.17.gain_ref = bf16[1,512]{1,0:T(2,128)(2,1)} reshape(bf16[512]{0:T(512)(128)(2,1)} %param.9) | data formatting | bytes 2048 | tf_op jit(solution)/shard_map/reshape | solution.py:350
  4.7 49.7 %shard_map.82 = bf16[4,512]{1,0:T(4,128)(2,1)} custom-call(s32[8,4]{1,0:T(8,128)} %copy.9.slab_ref, s32[4]{0:T(128)} %len_ref.1, bf16[4,512]{1,0:T(4,128)(2,1)} %hidden_ref.1, bf16[1,512]{1,0:T(2,128)(2,1)} %reshape.17.gain_ref, f32[24,128]{1,0:T(8,128)} %concatenate.13.cos_ref, f32[24,128]{1,0:T(8,128)} %concatenate.15.sin_ref, bf16[512,16384]{1,0:T(8,128)(2,1)} %wq_hbm.1, ...), custom_call_target="tpu_custom_call" | custom-call | tf_op jit(solution)/shard_map/pallas_call | solution.py:311
  54.5 1.3 %copy.11 = bf16[4,512]{1,0:T(4,128)(2,1)} copy(bf16[4,512]{1,0:T(4,128)(2,1)} %shard_map.82) | data formatting | bytes 8192
  (5 shorter events, 0.0 us)
